TPU v7x, 128 devices: a whole 4x4x4 slice. The times are simulated.
128 devices in a mesh: row: 16 (over y, z), col: 8 (over x, core).
Axes of the slice: x: 4, y: 4, z: 4, core: 2. Of those that a mesh axis runs over, the one named last changes fastest.
Arguments:
- grid_values: bfloat16 [512, 256, 384], P(('row', 'col')), may hold values from -0.109375 to 0.109375
- external: float32 [512, 256], P(('row', 'col')), may hold values from 0 to 6
- tiles: int32 [512, 3], P(('row', 'col')), may hold values from 0 to 15, as said below
- kinetic: bfloat16 [16384, 16384], P('row', 'col'), may hold values from -0.046875 to 0.046875
- orbitals: bfloat16 [16384, 256], P(('row', 'col')), may hold values from -6 to 6
Outputs:
- filtered: float32 [16384, 256], P(('row', 'col'))
Inputs may be any that keep to these rules, and one draw needn't show every extreme that they name: Each batch names 3 distinct tiles in increasing order. Among the 4 batches of one device no tile is named more than 2 times; in every draw some tile is named exactly 2 times by the batches of every device.
All inputs are finite; a program needn't handle non-finite values.
Results may differ from a plain program's by a relative error of at most 0.0064.
Values may be sent and summed in bfloat16 or wider, within the bound.
A program may use at most 128 MiB of HBM per device.

v0:
```python
import jax
import jax.numpy as jnp
from jax import lax
from jax.sharding import PartitionSpec as P

TILE = 128
LISTED = 3
LIST = 384
center = 1.0
spread = 2.5


def body(grid_values, external, tiles, kinetic, orbitals):
    row_count = lax.axis_size("row")
    shard_rows, orbital_count = orbitals.shape
    per_shard = shard_rows // TILE
    group_tiles = row_count * per_shard
    batch_count = tiles.shape[0]
    group_orbitals = lax.all_gather(orbitals, "row", axis=0, tiled=True)
    listed_orbitals = group_orbitals.reshape(group_tiles, TILE, orbital_count)[tiles].reshape(
        batch_count, LIST, orbital_count
    )
    waves = jnp.einsum(
        "bpl,blk->bpk", grid_values, listed_orbitals, preferred_element_type=jnp.float32
    )
    density = jnp.sum(waves * waves, axis=2)
    potential = external - jnp.cbrt(3.0 * density / jnp.pi)
    weighted = (potential[:, :, None] * grid_values).astype(jnp.bfloat16)
    integrals = jnp.einsum(
        "bpl,bpm->blm", grid_values, weighted, preferred_element_type=jnp.float32
    )
    blocks = integrals.reshape(batch_count, LISTED, TILE, LISTED, TILE).transpose(0, 1, 3, 2, 4)
    dense_local = (
        jnp.zeros((group_tiles, TILE, group_tiles, TILE), jnp.float32)
        .at[tiles[:, :, None], :, tiles[:, None, :], :]
        .add(blocks)
    )
    dense_local = dense_local.reshape(group_tiles * TILE, group_tiles * TILE)
    grid_rows = lax.psum_scatter(dense_local, "row", scatter_dimension=0, tiled=True)
    row_start = lax.axis_index("col") * shard_rows
    updated = (
        lax.dynamic_slice_in_dim(kinetic, row_start, shard_rows, 0).astype(jnp.float32) + grid_rows
    )
    hamiltonian = lax.dynamic_update_slice_in_dim(
        kinetic, updated.astype(jnp.bfloat16), row_start, 0
    )

    def add_piece(piece):
        return jnp.dot(hamiltonian, piece, preferred_element_type=jnp.float32)

    def times_ham(vectors):
        return add_piece(lax.all_gather(vectors, "row", axis=0, tiled=True))

    def filter_step(partial_value, vectors):
        reduced = lax.psum_scatter(partial_value, "col", scatter_dimension=0, tiled=True)
        return reduced / spread - center / spread * vectors.astype(jnp.float32)

    first_term = filter_step(
        jnp.dot(hamiltonian, group_orbitals, preferred_element_type=jnp.float32), orbitals
    ).astype(jnp.bfloat16)
    second_term = (
        2.0 * filter_step(times_ham(first_term), first_term) - orbitals.astype(jnp.float32)
    ).astype(jnp.bfloat16)
    return 2.0 * filter_step(times_ham(second_term), second_term) - first_term.astype(jnp.float32)


def solution(mesh):
    return jax.shard_map(
        body,
        mesh=mesh,
        in_specs=(
            P(("row", "col"), None, None),
            P(("row", "col"), None),
            P(("row", "col"), None),
            P("row", "col"),
            P(("row", "col"), None),
        ),
        out_specs=P(("row", "col"), None),
        check_vma=False,
    )
```

profile of v0, /device:TPU:0, one launch (start us, length us, event | category | flops | bytes accessed | tf_op | source)
XLA Modules:
  0.0 429.0 jit_solution(10878357735825306583)
XLA Ops:
  6.5 4.8 %copy.28 = bf16[1024,2048]{1,0:T(8,128)(2,1)} copy(bf16[1024,2048]{1,0:T(8,128)(2,1)} %param.8) | data formatting | bytes 8388608
  11.4 0.0 reduce-scatter.5.cloned.1.call-start
  11.5 0.1 or_select_fusion
  11.5 0.1 reshape.38
  11.6 0.1 reshape.32
  11.7 44.9 %all-gather.4.cloned.1.call-done = bf16[2048,256]{1,0:T(8,128)(2,1)} async-done(((bf16[128,256]{1,0:T(8,128)(2,1)}), bf16[2048,256]{1,0:T(8,128)(2,1)}) %all-gather.4.cloned.1.call-update) | async-done | bytes 1048592 | tf_op jit(solution)/shard_map/all_gather | solution.py:19
  56.7 1.8 gather_fusion
  58.5 0.5 fusion
  59.0 0.9 convolution_bitcast_fusion
  60.0 2.0 copy.17
  62.0 4.5 %reshape.28 = f32[4,3,128,3,128]{4,3,2,1,0:T(4,128)} reshape(f32[4,384,384]{2,1,0:T(8,128)} %copy.17) | data formatting | bytes 4718592 | tf_op jit(solution)/shard_map/reshape | solution.py:32
  66.5 2.2 copy.18
  68.7 7.9 %broadcast_in_dim.8 = f32[16,128,16,128]{3,1,2,0:T(8,128)} broadcast(f32[]{:T(128)} %constant.13.clone.1), dimensions={} | broadcast | bytes 16777220 | tf_op jit(solution)/shard_map/broadcast_in_dim | solution.py:34
  76.6 9.1 %scatter_fusion = f32[16,128,16,128]{3,1,2,0:T(8,128)} fusion(f32[16,128,16,128]{3,1,2,0:T(8,128)} %broadcast_in_dim.8, s32[36]{0:T(128)S(1)} %reshape.38, f32[36,128,128]{2,1,0:T(8,128)S(1)} %bitcast.24), kind=kCustom, calls=%fused_computation.1 | custom fusion | flops 589824 | bytes 7078176 | tf_op jit(solution)/shard_map/scatter-add | solution.py:36
  85.7 15.5 %copy.19 = f32[16,128,16,128]{3,2,1,0:T(8,128)S(1)} copy(f32[16,128,16,128]{3,1,2,0:T(8,128)} %scatter_fusion) | data formatting | bytes 33554432 | tf_op jit(solution)/shard_map/scatter-add | solution.py:36
  101.2 11.2 %copy.24 = f32[256,8,16,128]{3,1,2,0:T(8,128)} copy(f32[256,8,16,128]{3,2,1,0:T(8,128)S(1)} %bitcast.23) | data formatting | bytes 33554432
  112.4 0.2 reduce-scatter.7.cloned.1.call-start
  112.6 110.1 %reduce-scatter.5.cloned.1.call-done = f32[128,2048]{1,0:T(8,128)} async-done(((f32[2048,2048]{1,0:T(8,128)}), f32[128,2048]{1,0:T(8,128)}) %reduce-scatter.5.cloned.1.call-update) | async-done | bytes 1048592 | tf_op jit(solution)/shard_map/reduce_scatter | solution.py:39
  222.8 2.3 fusion.2
  225.1 4.4 %fusion.8 = f32[1024,256]{1,0:T(8,128)} fusion(bf16[1024,2048]{1,0:T(8,128)(2,1)} %fusion.2, bf16[2048,256]{1,0:T(8,128)(2,1)S(1)} %copy-done.2), kind=kOutput, calls=%fused_computation.26 | convolution fusion | flops 1073741824 | bytes 6291456 | tf_op jit(solution)/shard_map/dot_general | solution.py:59
  229.5 0.0 all-gather.6.cloned.1.call-start
  229.6 31.5 %reduce-scatter.7.cloned.1.call-done = f32[128,256]{1,0:T(8,128)} async-done(((f32[1024,256]{1,0:T(8,128)}), f32[128,256]{1,0:T(8,128)}) %reduce-scatter.7.cloned.1.call-update) | async-done | bytes 131088 | tf_op jit(solution)/shard_map/reduce_scatter | solution.py:55
  261.1 1.6 fusion.4
  262.7 0.0 reduce-scatter.9.cloned.1.call-start
  262.7 41.8 %all-gather.6.cloned.1.call-done = bf16[2048,256]{1,0:T(8,128)(2,1)} async-done(((bf16[128,256]{1,0:T(8,128)(2,1)}), bf16[2048,256]{1,0:T(8,128)(2,1)}) %all-gather.6.cloned.1.call-update) | async-done | bytes 1048592 | tf_op jit(solution)/shard_map/all_gather | solution.py:52
  304.5 4.7 %fusion.9 = f32[1024,256]{1,0:T(8,128)} fusion(bf16[1024,2048]{1,0:T(8,128)(2,1)} %fusion.2, bf16[2048,256]{1,0:T(8,128)(2,1)} %all-gather.6.cloned.1.call-done), kind=kOutput, calls=%fused_computation.27 | convolution fusion | flops 1073741824 | bytes 6291456 | tf_op jit(solution)/shard_map/dot_general | solution.py:49
  309.3 31.5 %reduce-scatter.9.cloned.1.call-done = f32[128,256]{1,0:T(8,128)} async-done(((f32[1024,256]{1,0:T(8,128)}), f32[128,256]{1,0:T(8,128)}) %reduce-scatter.9.cloned.1.call-update) | async-done | bytes 131088 | tf_op jit(solution)/shard_map/reduce_scatter | solution.py:55
  340.8 1.6 fusion.5
  342.5 41.9 %all-gather.8.cloned.1.call-done = bf16[2048,256]{1,0:T(8,128)(2,1)} async-done(((bf16[128,256]{1,0:T(8,128)(2,1)}), bf16[2048,256]{1,0:T(8,128)(2,1)}) %all-gather.8.cloned.1.call-update) | async-done | bytes 1048592 | tf_op jit(solution)/shard_map/all_gather | solution.py:52
  384.3 4.7 %fusion.10 = f32[1024,256]{1,0:T(8,128)} fusion(bf16[1024,2048]{1,0:T(8,128)(2,1)} %fusion.2, bf16[2048,256]{1,0:T(8,128)(2,1)} %all-gather.8.cloned.1.call-done), kind=kOutput, calls=%fused_computation.28 | convolution fusion | flops 1073741824 | bytes 6291456 | tf_op jit(solution)/shard_map/dot_general | solution.py:49
  389.1 31.5 %reduce-scatter.11.cloned.1.call-done = f32[128,256]{1,0:T(8,128)} async-done(((f32[1024,256]{1,0:T(8,128)}), f32[128,256]{1,0:T(8,128)}) %reduce-scatter.11.cloned.1.call-update) | async-done | bytes 131088 | tf_op jit(solution)/shard_map/reduce_scatter | solution.py:55
  420.6 1.6 convert_subtract_fusion
  (28 shorter events, 0.3 us)
Async XLA Ops:
  6.5 4.9 %copy-start.5 = (s32[4,3]{1,0:T(4,128)S(1)}, s32[4,3]{1,0:T(4,128)}, u32[]{:S(2)}) copy-start(s32[4,3]{1,0:T(4,128)} %param.7) | copy-start | bytes 148
  6.5 52.0 %copy-start = (bf16[4,256,384]{2,1,0:T(8,128)(2,1)S(1)}, bf16[4,256,384]{2,1,0:T(8,128)(2,1)}, u32[]{:S(2)}) copy-start(bf16[4,256,384]{2,1,0:T(8,128)(2,1)} %param.5) | copy-start | bytes 2359300
  6.5 52.5 %copy-start.6 = (f32[4,256]{1,0:T(4,128)S(1)}, f32[4,256]{1,0:T(4,128)}, u32[]{:S(2)}) copy-start(f32[4,256]{1,0:T(4,128)} %param.6) | copy-start | bytes 12292
  6.5 50.1 %all-gather.4.cloned.1.call-start = ((), (), s32[]{:S(2)}) async-start(), calls=%async_computation.4 | async-start | bytes 1114112 | tf_op jit(solution)/shard_map/all_gather | solution.py:19
  11.4 211.4 %reduce-scatter.5.cloned.1.call-start = ((), (), s32[]{:S(2)}) async-start(), calls=%async_computation.5 | async-start | bytes 17825792 | tf_op jit(solution)/shard_map/reduce_scatter | solution.py:39
  112.4 112.7 %copy-start.2 = (bf16[2048,256]{1,0:T(8,128)(2,1)S(1)}, bf16[2048,256]{1,0:T(8,128)(2,1)}, u32[]{:S(2)}) copy-start(bf16[2048,256]{1,0:T(8,128)(2,1)} %all-gather.4.cloned.1.call-done) | copy-start | bytes 3145732
  112.4 148.7 %reduce-scatter.7.cloned.1.call-start = ((), (), s32[]{:S(2)}) async-start(), calls=%async_computation.6 | async-start | bytes 1179648 | tf_op jit(solution)/shard_map/reduce_scatter | solution.py:55
  225.0 36.0 %copy-start.3 = (bf16[128,256]{1,0:T(8,128)(2,1)S(1)}, bf16[128,256]{1,0:T(8,128)(2,1)}, u32[]{:S(2)}) copy-start(bf16[128,256]{1,0:T(8,128)(2,1)} %param.9) | copy-start | bytes 196612
  229.5 75.0 %all-gather.6.cloned.1.call-start = ((), (), s32[]{:S(2)}) async-start(), calls=%async_computation.7 | async-start | bytes 1114112 | tf_op jit(solution)/shard_map/all_gather | solution.py:52
  262.6 78.2 %copy-start.1 = (bf16[128,256]{1,0:T(8,128)(2,1)S(1)}, bf16[128,256]{1,0:T(8,128)(2,1)}, u32[]{:S(2)}) copy-start(bf16[128,256]{1,0:T(8,128)(2,1)} %fusion.4) | copy-start | bytes 196612
  262.7 78.1 %reduce-scatter.9.cloned.1.call-start = ((), (), s32[]{:S(2)}) async-start(), calls=%async_computation.8 | async-start | bytes 1179648 | tf_op jit(solution)/shard_map/reduce_scatter | solution.py:55
  309.3 75.1 %all-gather.8.cloned.1.call-start = ((), (), s32[]{:S(2)}) async-start(), calls=%async_computation.9 | async-start | bytes 1114112 | tf_op jit(solution)/shard_map/all_gather | solution.py:52
  342.4 78.2 %copy-start.4 = (bf16[128,256]{1,0:T(8,128)(2,1)S(1)}, bf16[128,256]{1,0:T(8,128)(2,1)}, u32[]{:S(2)}) copy-start(bf16[128,256]{1,0:T(8,128)(2,1)} %fusion.5) | copy-start | bytes 196612
  342.4 78.2 %reduce-scatter.11.cloned.1.call-start = ((), (), s32[]{:S(2)}) async-start(), calls=%async_computation.10 | async-start | bytes 1179648 | tf_op jit(solution)/shard_map/reduce_scatter | solution.py:55
Sparse Core Ops, SparseCore 0:
  11.5 45.1 all-gather.3
  112.5 110.1 reduce-scatter.4
  229.6 31.3 reduce-scatter.6
  263.1 41.4 all-gather.5
  309.4 31.3 reduce-scatter.8
  342.8 41.4 all-gather.7
  389.2 31.3 reduce-scatter.10
where the time goes:
time: 430 us; the launch traced here: 429 us
  waiting for transfers between devices  333 us (77%)
  local copies, waits for them, and re-layouts  50.1 us (12%)
  other arithmetic  16.3 us (4%)
  matrix products  15.3 us (4%)
  between operations  13.6 us (3%)
    reduce_scatter x1, waiting for transfers between devices, body(): lax.psum_scatter(dense_local, 'row', scatter_dimension=0, tiled=True)  110 us
    reduce_scatter x3, waiting for transfers between devices, filter_step(): lax.psum_scatter(partial_value, 'col', scatter_dimension=0, tiled=True)  94.5 us
    all_gather x2, waiting for transfers between devices, times_ham(): return add_piece(lax.all_gather(vectors, 'row', axis=0, tiled=True))  83.7 us
    all_gather x1, waiting for transfers between devices, body(): group_orbitals = lax.all_gather(orbitals, 'row', axis=0, tiled=True)  44.9 us
    unnamed x16, local copies, waits for them, and re-layouts  16 us
    scatter-add x1, local copies, waits for them, and re-layouts, body(): dense_local = jnp.zeros((group_tiles, TILE, group_tiles, TILE), jnp.float...  15.5 us
    dot_general x2, matrix products, add_piece(): return jnp.dot(hamiltonian, piece, preferred_element_type=jnp.float32)  9.42 us
    scatter-add x1, other arithmetic, body(): dense_local = jnp.zeros((group_tiles, TILE, group_tiles, TILE), jnp.float...  9.12 us
  transfers between devices with their start and end apart: 7, of which 7 were waited for; matrix products, arithmetic and copies ran while one was open for 0% of the time, Pallas kernels for 0%

commit v1 on v0

--- a/solution.py
+++ b/solution.py
@@ -10,13 +10,26 @@
 spread = 2.5
 
 
+def gather_around(shard, axis, dim):
+    ways = lax.axis_size(axis)
+    up = [(d, (d + 1) % ways) for d in range(ways)]
+    down = [(d, (d - 1) % ways) for d in range(ways)]
+    earlier, later = ([shard], [shard])
+    for _ in range(ways // 2):
+        earlier.append(lax.ppermute(earlier[-1], axis, up))
+    for _ in range((ways - 1) // 2):
+        later.append(lax.ppermute(later[-1], axis, down))
+    line = jnp.concatenate([*earlier[::-1], *later[1:]], axis=dim)
+    return jnp.roll(line, (lax.axis_index(axis) - ways // 2) * shard.shape[dim], axis=dim)
+
+
 def body(grid_values, external, tiles, kinetic, orbitals):
     row_count = lax.axis_size("row")
     shard_rows, orbital_count = orbitals.shape
     per_shard = shard_rows // TILE
     group_tiles = row_count * per_shard
     batch_count = tiles.shape[0]
-    group_orbitals = lax.all_gather(orbitals, "row", axis=0, tiled=True)
+    group_orbitals = gather_around(orbitals, "row", 0)
     listed_orbitals = group_orbitals.reshape(group_tiles, TILE, orbital_count)[tiles].reshape(
         batch_count, LIST, orbital_count
     )

time: 430 us -> 450 us (1.047)
  starting transfers between devices: 0.43 us -> 40.2 us
  waiting for transfers between devices: 333 us -> 313 us
    all_gather x1 -> x0, waiting for transfers between devices: 44.9 us -> none  [body(): group_orbitals = lax.all_gather(orbitals, 'row', axis=0, tiled=True)]
    ppermute x0 -> x15, starting transfers between devices: none -> 40 us  [the longest x7 37.9 us: gather_around(): later.append(lax.ppermute(later[-1], axis, down))]
    ppermute x0 -> x15, waiting for transfers between devices: none -> 22.2 us  [the longest x8 22.2 us: gather_around(): earlier.append(lax.ppermute(earlier[-1], axis, up))]
    unnamed x16 -> x45, local copies, waits for them, and re-layouts: 16 us -> 16.5 us
  transfers between devices with their start and end apart: 7 -> 21, of which waited for: 7 -> 14; matrix products, arithmetic and copies ran while one was open for 0% -> 0% of each run, Pallas kernels for 0% -> 0%
where the time goes in v1:
time: 450 us; the launch traced here: 449 us
  waiting for transfers between devices  313 us (70%)
  local copies, waits for them, and re-layouts  49.4 us (11%)
  starting transfers between devices  40.2 us (9%)
  matrix products  16.7 us (4%)
  other arithmetic  16.4 us (4%)
  between operations  13.9 us (3%)
    reduce_scatter x1, waiting for transfers between devices, body(): lax.psum_scatter(dense_local, 'row', scatter_dimension=0, tiled=True)  112 us
    reduce_scatter x3, waiting for transfers between devices, filter_step(): lax.psum_scatter(partial_value, 'col', scatter_dimension=0, tiled=True)  94.4 us
    all_gather x2, waiting for transfers between devices, times_ham(): return add_piece(lax.all_gather(vectors, 'row', axis=0, tiled=True))  84 us
    ppermute x7, starting transfers between devices, gather_around(): later.append(lax.ppermute(later[-1], axis, down))  37.9 us
    ppermute x8, waiting for transfers between devices, gather_around(): earlier.append(lax.ppermute(earlier[-1], axis, up))  22.2 us
    unnamed x45, local copies, waits for them, and re-layouts  16.5 us
    scatter-add x1, local copies, waits for them, and re-layouts, body(): dense_local = jnp.zeros((group_tiles, TILE, group_tiles, TILE), jnp.float...  15.5 us
    dot_general x2, matrix products, add_piece(): return jnp.dot(hamiltonian, piece, preferred_element_type=jnp.float32)  9.48 us
  transfers between devices with their start and end apart: 21, of which 14 were waited for; matrix products, arithmetic and copies ran while one was open for 0% of the time, Pallas kernels for 0%

profile of v1, /device:TPU:0, one launch (start us, length us, event | category | flops | bytes accessed | tf_op | source)
XLA Modules:
  0.0 449.5 jit_solution(17173363061983561110)
XLA Ops:
  6.5 4.7 %copy.59 = bf16[1024,2048]{1,0:T(8,128)(2,1)} copy(bf16[1024,2048]{1,0:T(8,128)(2,1)} %param.8) | data formatting | bytes 8388608
  11.3 2.0 collective-permute-start
  13.3 6.8 %collective-permute-done = bf16[128,256]{1,0:T(8,128)(2,1)S(1)} collective-permute-done((bf16[128,256]{1,0:T(8,128)(2,1)S(1)}, bf16[128,256]{1,0:T(8,128)(2,1)S(1)}, u32[]{:S(2)}, u32[]{:S(2)}) %collective-permute-start) | collective-permute-done | bytes 65568 | tf_op jit(solution)/shard_map/ppermute | solution.py:19
  20.1 5.3 %collective-permute-start.8 = (bf16[128,256]{1,0:T(8,128)(2,1)S(1)}, bf16[128,256]{1,0:T(8,128)(2,1)S(1)}, u32[]{:S(2)}, u32[]{:S(2)}) collective-permute-start(bf16[128,256]{1,0:T(8,128)(2,1)S(1)} %copy-done.1), channel_id=1, source_target_pairs={{0,120},{8,0},{16,8},{24,16},{32,24},{40,32},{48,40},{56,48},{64,5... | collective-permute-start | bytes 196616 | tf_op jit(solution)/shard_map/ppermute | solution.py:21
  25.5 2.2 collective-permute-done.1
  27.7 5.3 %collective-permute-start.9 = (bf16[128,256]{1,0:T(8,128)(2,1)S(1)}, bf16[128,256]{1,0:T(8,128)(2,1)S(1)}, u32[]{:S(2)}, u32[]{:S(2)}) collective-permute-start(bf16[128,256]{1,0:T(8,128)(2,1)S(1)} %collective-permute-done.8), channel_id=1, source_target_pairs={{0,120},{8,0},{16,8},{24,16},{32,24},{40,32},{48,40},{56,48},{64,5... | collective-permute-start | bytes 196616 | tf_op jit(solution)/shard_map/ppermute | solution.py:21
  33.1 2.2 collective-permute-done.2
  35.3 5.3 %collective-permute-start.10 = (bf16[128,256]{1,0:T(8,128)(2,1)S(1)}, bf16[128,256]{1,0:T(8,128)(2,1)S(1)}, u32[]{:S(2)}, u32[]{:S(2)}) collective-permute-start(bf16[128,256]{1,0:T(8,128)(2,1)S(1)} %collective-permute-done.9), channel_id=1, source_target_pairs={{0,120},{8,0},{16,8},{24,16},{32,24},{40,32},{48,40},{56,48},{64,5... | collective-permute-start | bytes 196616 | tf_op jit(solution)/shard_map/ppermute | solution.py:21
  40.6 2.2 collective-permute-done.3
  42.9 5.4 %collective-permute-start.11 = (bf16[128,256]{1,0:T(8,128)(2,1)S(1)}, bf16[128,256]{1,0:T(8,128)(2,1)S(1)}, u32[]{:S(2)}, u32[]{:S(2)}) collective-permute-start(bf16[128,256]{1,0:T(8,128)(2,1)S(1)} %collective-permute-done.10), channel_id=1, source_target_pairs={{0,120},{8,0},{16,8},{24,16},{32,24},{40,32},{48,40},{56,48},{64,5... | collective-permute-start | bytes 196616 | tf_op jit(solution)/shard_map/ppermute | solution.py:21
  48.3 2.1 collective-permute-done.4
  50.5 5.4 %collective-permute-start.12 = (bf16[128,256]{1,0:T(8,128)(2,1)S(1)}, bf16[128,256]{1,0:T(8,128)(2,1)S(1)}, u32[]{:S(2)}, u32[]{:S(2)}) collective-permute-start(bf16[128,256]{1,0:T(8,128)(2,1)S(1)} %collective-permute-done.11), channel_id=1, source_target_pairs={{0,120},{8,0},{16,8},{24,16},{32,24},{40,32},{48,40},{56,48},{64,5... | collective-permute-start | bytes 196616 | tf_op jit(solution)/shard_map/ppermute | solution.py:21
  55.9 2.7 collective-permute-done.5
  58.9 5.4 %collective-permute-start.13 = (bf16[128,256]{1,0:T(8,128)(2,1)S(1)}, bf16[128,256]{1,0:T(8,128)(2,1)S(1)}, u32[]{:S(2)}, u32[]{:S(2)}) collective-permute-start(bf16[128,256]{1,0:T(8,128)(2,1)S(1)} %collective-permute-done.12), channel_id=1, source_target_pairs={{0,120},{8,0},{16,8},{24,16},{32,24},{40,32},{48,40},{56,48},{64,5... | collective-permute-start | bytes 196616 | tf_op jit(solution)/shard_map/ppermute | solution.py:21
  66.2 5.7 %collective-permute-start.14 = (bf16[128,256]{1,0:T(8,128)(2,1)S(1)}, bf16[128,256]{1,0:T(8,128)(2,1)S(1)}, u32[]{:S(2)}, u32[]{:S(2)}) collective-permute-start(bf16[128,256]{1,0:T(8,128)(2,1)S(1)} %collective-permute-done.13), channel_id=1, source_target_pairs={{0,120},{8,0},{16,8},{24,16},{32,24},{40,32},{48,40},{56,48},{64,5... | collective-permute-start | bytes 196616 | tf_op jit(solution)/shard_map/ppermute | solution.py:21
  75.9 2.3 convolution_bitcast_fusion
  80.2 4.6 %reshape.28 = f32[4,3,128,3,128]{4,3,2,1,0:T(4,128)} reshape(f32[4,384,384]{2,1,0:T(8,128)} %copy.17) | data formatting | bytes 4718592 | tf_op jit(solution)/shard_map/reshape | solution.py:45
  84.7 2.2 copy.18
  86.9 7.9 %broadcast_in_dim.8 = f32[16,128,16,128]{3,1,2,0:T(8,128)} broadcast(f32[]{:T(128)} %constant.51.clone.1), dimensions={} | broadcast | bytes 16777220 | tf_op jit(solution)/shard_map/broadcast_in_dim | solution.py:47
  94.8 9.3 %scatter_fusion = f32[16,128,16,128]{3,1,2,0:T(8,128)} fusion(f32[16,128,16,128]{3,1,2,0:T(8,128)} %broadcast_in_dim.8, s32[36]{0:T(128)S(1)} %reshape.38, f32[36,128,128]{2,1,0:T(8,128)S(1)} %bitcast.24), kind=kCustom, calls=%fused_computation.1 | custom fusion | flops 589824 | bytes 7078176 | tf_op jit(solution)/shard_map/scatter-add | solution.py:49
  104.0 15.5 %copy.19 = f32[16,128,16,128]{3,2,1,0:T(8,128)S(1)} copy(f32[16,128,16,128]{3,1,2,0:T(8,128)} %scatter_fusion) | data formatting | bytes 33554432 | tf_op jit(solution)/shard_map/scatter-add | solution.py:49
  119.5 11.2 %copy.24 = f32[256,8,16,128]{3,1,2,0:T(8,128)} copy(f32[256,8,16,128]{3,2,1,0:T(8,128)S(1)} %bitcast.23) | data formatting | bytes 33554432
  130.8 112.1 %reduce-scatter.5.cloned.1.call-done = f32[128,2048]{1,0:T(8,128)} async-done(((f32[2048,2048]{1,0:T(8,128)}), f32[128,2048]{1,0:T(8,128)}) %reduce-scatter.5.cloned.1.call-update) | async-done | bytes 1048592 | tf_op jit(solution)/shard_map/reduce_scatter | solution.py:52
  242.9 2.3 fusion.2
  245.2 4.4 fusion.8
  249.7 31.4 %reduce-scatter.7.cloned.1.call-done = f32[128,256]{1,0:T(8,128)} async-done(((f32[1024,256]{1,0:T(8,128)}), f32[128,256]{1,0:T(8,128)}) %reduce-scatter.7.cloned.1.call-update) | async-done | bytes 131088 | tf_op jit(solution)/shard_map/reduce_scatter | solution.py:68
  282.8 42.1 %all-gather.3.cloned.1.call-done = bf16[2048,256]{1,0:T(8,128)(2,1)} async-done(((bf16[128,256]{1,0:T(8,128)(2,1)}), bf16[2048,256]{1,0:T(8,128)(2,1)}) %all-gather.3.cloned.1.call-update) | async-done | bytes 1048592 | tf_op jit(solution)/shard_map/all_gather | solution.py:65
  324.8 4.7 %fusion.9 = f32[1024,256]{1,0:T(8,128)} fusion(bf16[1024,2048]{1,0:T(8,128)(2,1)} %fusion.2, bf16[2048,256]{1,0:T(8,128)(2,1)} %all-gather.3.cloned.1.call-done), kind=kOutput, calls=%fused_computation.60 | convolution fusion | flops 1073741824 | bytes 6291456 | tf_op jit(solution)/shard_map/dot_general | solution.py:62
  329.6 31.5 %reduce-scatter.9.cloned.1.call-done = f32[128,256]{1,0:T(8,128)} async-done(((f32[1024,256]{1,0:T(8,128)}), f32[128,256]{1,0:T(8,128)}) %reduce-scatter.9.cloned.1.call-update) | async-done | bytes 131088 | tf_op jit(solution)/shard_map/reduce_scatter | solution.py:68
  362.8 41.9 %all-gather.5.cloned.1.call-done = bf16[2048,256]{1,0:T(8,128)(2,1)} async-done(((bf16[128,256]{1,0:T(8,128)(2,1)}), bf16[2048,256]{1,0:T(8,128)(2,1)}) %all-gather.5.cloned.1.call-update) | async-done | bytes 1048592 | tf_op jit(solution)/shard_map/all_gather | solution.py:65
  404.7 4.7 %fusion.10 = f32[1024,256]{1,0:T(8,128)} fusion(bf16[1024,2048]{1,0:T(8,128)(2,1)} %fusion.2, bf16[2048,256]{1,0:T(8,128)(2,1)} %all-gather.5.cloned.1.call-done), kind=kOutput, calls=%fused_computation.61 | convolution fusion | flops 1073741824 | bytes 6291456 | tf_op jit(solution)/shard_map/dot_general | solution.py:62
  409.5 31.5 %reduce-scatter.11.cloned.1.call-done = f32[128,256]{1,0:T(8,128)} async-done(((f32[1024,256]{1,0:T(8,128)}), f32[128,256]{1,0:T(8,128)}) %reduce-scatter.11.cloned.1.call-update) | async-done | bytes 131088 | tf_op jit(solution)/shard_map/reduce_scatter | solution.py:68
  (86 shorter events, 12.9 us)
Async XLA Ops:
  6.5 4.7 %copy-start.1 = (bf16[128,256]{1,0:T(8,128)(2,1)S(1)}, bf16[128,256]{1,0:T(8,128)(2,1)}, u32[]{:S(2)}) copy-start(bf16[128,256]{1,0:T(8,128)(2,1)} %param.9) | copy-start | bytes 196612
  6.5 36.4 %copy-start.4 = (s32[4,3]{1,0:T(4,128)S(1)}, s32[4,3]{1,0:T(4,128)}, u32[]{:S(2)}) copy-start(s32[4,3]{1,0:T(4,128)} %param.7) | copy-start | bytes 148
  6.5 236.4 %reduce-scatter.5.cloned.1.call-start = ((), (), s32[]{:S(2)}) async-start(), calls=%async_computation.4 | async-start | bytes 17825792 | tf_op jit(solution)/shard_map/reduce_scatter | solution.py:52
  11.3 8.8 %collective-permute-start = (bf16[128,256]{1,0:T(8,128)(2,1)S(1)}, bf16[128,256]{1,0:T(8,128)(2,1)S(1)}, u32[]{:S(2)}, u32[]{:S(2)}) collective-permute-start(bf16[128,256]{1,0:T(8,128)(2,1)S(1)} %copy-done.1), channel_id=1, source_target_pairs={{0,8},{8,16},{16,24},{24,32},{32,40},{40,48},{48,56},{56,64},{64,7... | collective-permute-start | bytes 196616 | tf_op jit(solution)/shard_map/ppermute | solution.py:19
  20.1 7.6 %collective-permute-start.1 = (bf16[128,256]{1,0:T(8,128)(2,1)S(1)}, bf16[128,256]{1,0:T(8,128)(2,1)S(1)}, u32[]{:S(2)}, u32[]{:S(2)}) collective-permute-start(bf16[128,256]{1,0:T(8,128)(2,1)S(1)} %collective-permute-done), channel_id=1, source_target_pairs={{0,8},{8,16},{16,24},{24,32},{32,40},{40,48},{48,56},{56,64},{64,7... | collective-permute-start | bytes 196616 | tf_op jit(solution)/shard_map/ppermute | solution.py:19
  20.1 7.6 %collective-permute-start.8 = (bf16[128,256]{1,0:T(8,128)(2,1)S(1)}, bf16[128,256]{1,0:T(8,128)(2,1)S(1)}, u32[]{:S(2)}, u32[]{:S(2)}) collective-permute-start(bf16[128,256]{1,0:T(8,128)(2,1)S(1)} %copy-done.1), channel_id=1, source_target_pairs={{0,120},{8,0},{16,8},{24,16},{32,24},{40,32},{48,40},{56,48},{64,5... | collective-permute-start | bytes 196616 | tf_op jit(solution)/shard_map/ppermute | solution.py:21
  27.7 7.6 %collective-permute-start.2 = (bf16[128,256]{1,0:T(8,128)(2,1)S(1)}, bf16[128,256]{1,0:T(8,128)(2,1)S(1)}, u32[]{:S(2)}, u32[]{:S(2)}) collective-permute-start(bf16[128,256]{1,0:T(8,128)(2,1)S(1)} %collective-permute-done.1), channel_id=1, source_target_pairs={{0,8},{8,16},{16,24},{24,32},{32,40},{40,48},{48,56},{56,64},{64,7... | collective-permute-start | bytes 196616 | tf_op jit(solution)/shard_map/ppermute | solution.py:19
  27.7 7.6 %collective-permute-start.9 = (bf16[128,256]{1,0:T(8,128)(2,1)S(1)}, bf16[128,256]{1,0:T(8,128)(2,1)S(1)}, u32[]{:S(2)}, u32[]{:S(2)}) collective-permute-start(bf16[128,256]{1,0:T(8,128)(2,1)S(1)} %collective-permute-done.8), channel_id=1, source_target_pairs={{0,120},{8,0},{16,8},{24,16},{32,24},{40,32},{48,40},{56,48},{64,5... | collective-permute-start | bytes 196616 | tf_op jit(solution)/shard_map/ppermute | solution.py:21
  35.3 7.6 %collective-permute-start.3 = (bf16[128,256]{1,0:T(8,128)(2,1)S(1)}, bf16[128,256]{1,0:T(8,128)(2,1)S(1)}, u32[]{:S(2)}, u32[]{:S(2)}) collective-permute-start(bf16[128,256]{1,0:T(8,128)(2,1)S(1)} %collective-permute-done.2), channel_id=1, source_target_pairs={{0,8},{8,16},{16,24},{24,32},{32,40},{40,48},{48,56},{56,64},{64,7... | collective-permute-start | bytes 196616 | tf_op jit(solution)/shard_map/ppermute | solution.py:19
  35.3 7.6 %collective-permute-start.10 = (bf16[128,256]{1,0:T(8,128)(2,1)S(1)}, bf16[128,256]{1,0:T(8,128)(2,1)S(1)}, u32[]{:S(2)}, u32[]{:S(2)}) collective-permute-start(bf16[128,256]{1,0:T(8,128)(2,1)S(1)} %collective-permute-done.9), channel_id=1, source_target_pairs={{0,120},{8,0},{16,8},{24,16},{32,24},{40,32},{48,40},{56,48},{64,5... | collective-permute-start | bytes 196616 | tf_op jit(solution)/shard_map/ppermute | solution.py:21
  42.9 7.6 %collective-permute-start.4 = (bf16[128,256]{1,0:T(8,128)(2,1)S(1)}, bf16[128,256]{1,0:T(8,128)(2,1)S(1)}, u32[]{:S(2)}, u32[]{:S(2)}) collective-permute-start(bf16[128,256]{1,0:T(8,128)(2,1)S(1)} %collective-permute-done.3), channel_id=1, source_target_pairs={{0,8},{8,16},{16,24},{24,32},{32,40},{40,48},{48,56},{56,64},{64,7... | collective-permute-start | bytes 196616 | tf_op jit(solution)/shard_map/ppermute | solution.py:19
  42.9 7.6 %collective-permute-start.11 = (bf16[128,256]{1,0:T(8,128)(2,1)S(1)}, bf16[128,256]{1,0:T(8,128)(2,1)S(1)}, u32[]{:S(2)}, u32[]{:S(2)}) collective-permute-start(bf16[128,256]{1,0:T(8,128)(2,1)S(1)} %collective-permute-done.10), channel_id=1, source_target_pairs={{0,120},{8,0},{16,8},{24,16},{32,24},{40,32},{48,40},{56,48},{64,5... | collective-permute-start | bytes 196616 | tf_op jit(solution)/shard_map/ppermute | solution.py:21
  50.5 8.1 %collective-permute-start.5 = (bf16[128,256]{1,0:T(8,128)(2,1)S(1)}, bf16[128,256]{1,0:T(8,128)(2,1)S(1)}, u32[]{:S(2)}, u32[]{:S(2)}) collective-permute-start(bf16[128,256]{1,0:T(8,128)(2,1)S(1)} %collective-permute-done.4), channel_id=1, source_target_pairs={{0,8},{8,16},{16,24},{24,32},{32,40},{40,48},{48,56},{56,64},{64,7... | collective-permute-start | bytes 196616 | tf_op jit(solution)/shard_map/ppermute | solution.py:19
  50.5 8.4 %collective-permute-start.12 = (bf16[128,256]{1,0:T(8,128)(2,1)S(1)}, bf16[128,256]{1,0:T(8,128)(2,1)S(1)}, u32[]{:S(2)}, u32[]{:S(2)}) collective-permute-start(bf16[128,256]{1,0:T(8,128)(2,1)S(1)} %collective-permute-done.11), channel_id=1, source_target_pairs={{0,120},{8,0},{16,8},{24,16},{32,24},{40,32},{48,40},{56,48},{64,5... | collective-permute-start | bytes 196616 | tf_op jit(solution)/shard_map/ppermute | solution.py:21
  58.6 7.6 %collective-permute-start.6 = (bf16[128,256]{1,0:T(8,128)(2,1)S(1)}, bf16[128,256]{1,0:T(8,128)(2,1)S(1)}, u32[]{:S(2)}, u32[]{:S(2)}) collective-permute-start(bf16[128,256]{1,0:T(8,128)(2,1)S(1)} %collective-permute-done.5), channel_id=1, source_target_pairs={{0,8},{8,16},{16,24},{24,32},{32,40},{40,48},{48,56},{56,64},{64,7... | collective-permute-start | bytes 196616 | tf_op jit(solution)/shard_map/ppermute | solution.py:19
  58.9 7.3 %collective-permute-start.13 = (bf16[128,256]{1,0:T(8,128)(2,1)S(1)}, bf16[128,256]{1,0:T(8,128)(2,1)S(1)}, u32[]{:S(2)}, u32[]{:S(2)}) collective-permute-start(bf16[128,256]{1,0:T(8,128)(2,1)S(1)} %collective-permute-done.12), channel_id=1, source_target_pairs={{0,120},{8,0},{16,8},{24,16},{32,24},{40,32},{48,40},{56,48},{64,5... | collective-permute-start | bytes 196616 | tf_op jit(solution)/shard_map/ppermute | solution.py:21
  66.2 7.6 %collective-permute-start.7 = (bf16[128,256]{1,0:T(8,128)(2,1)S(1)}, bf16[128,256]{1,0:T(8,128)(2,1)S(1)}, u32[]{:S(2)}, u32[]{:S(2)}) collective-permute-start(bf16[128,256]{1,0:T(8,128)(2,1)S(1)} %collective-permute-done.6), channel_id=1, source_target_pairs={{0,8},{8,16},{16,24},{24,32},{32,40},{40,48},{48,56},{56,64},{64,7... | collective-permute-start | bytes 196616 | tf_op jit(solution)/shard_map/ppermute | solution.py:19
  66.2 7.8 %collective-permute-start.14 = (bf16[128,256]{1,0:T(8,128)(2,1)S(1)}, bf16[128,256]{1,0:T(8,128)(2,1)S(1)}, u32[]{:S(2)}, u32[]{:S(2)}) collective-permute-start(bf16[128,256]{1,0:T(8,128)(2,1)S(1)} %collective-permute-done.13), channel_id=1, source_target_pairs={{0,120},{8,0},{16,8},{24,16},{32,24},{40,32},{48,40},{56,48},{64,5... | collective-permute-start | bytes 196616 | tf_op jit(solution)/shard_map/ppermute | solution.py:21
  74.2 1.1 copy-start
  74.3 1.5 copy-start.5
  130.7 150.4 %reduce-scatter.7.cloned.1.call-start = ((), (), s32[]{:S(2)}) async-start(), calls=%async_computation.5 | async-start | bytes 1179648 | tf_op jit(solution)/shard_map/reduce_scatter | solution.py:68
  249.7 75.2 %all-gather.3.cloned.1.call-start = ((), (), s32[]{:S(2)}) async-start(), calls=%async_computation.6 | async-start | bytes 1114112 | tf_op jit(solution)/shard_map/all_gather | solution.py:65
  282.7 78.4 %copy-start.2 = (bf16[128,256]{1,0:T(8,128)(2,1)S(1)}, bf16[128,256]{1,0:T(8,128)(2,1)}, u32[]{:S(2)}) copy-start(bf16[128,256]{1,0:T(8,128)(2,1)} %fusion.4) | copy-start | bytes 196612
  282.7 78.4 %reduce-scatter.9.cloned.1.call-start = ((), (), s32[]{:S(2)}) async-start(), calls=%async_computation.7 | async-start | bytes 1179648 | tf_op jit(solution)/shard_map/reduce_scatter | solution.py:68
  329.6 75.1 %all-gather.5.cloned.1.call-start = ((), (), s32[]{:S(2)}) async-start(), calls=%async_computation.8 | async-start | bytes 1114112 | tf_op jit(solution)/shard_map/all_gather | solution.py:65
  362.7 78.3 %copy-start.3 = (bf16[128,256]{1,0:T(8,128)(2,1)S(1)}, bf16[128,256]{1,0:T(8,128)(2,1)}, u32[]{:S(2)}) copy-start(bf16[128,256]{1,0:T(8,128)(2,1)} %fusion.5) | copy-start | bytes 196612
  362.8 78.3 %reduce-scatter.11.cloned.1.call-start = ((), (), s32[]{:S(2)}) async-start(), calls=%async_computation.9 | async-start | bytes 1179648 | tf_op jit(solution)/shard_map/reduce_scatter | solution.py:68
Sparse Core Ops, SparseCore 0:
  130.8 112.0 reduce-scatter.4
  249.8 31.2 reduce-scatter.6
  283.3 41.5 all-gather.2
  329.7 31.3 reduce-scatter.8
  363.1 41.5 all-gather.4
  409.6 31.3 reduce-scatter.10
